TPU v7x, 512 devices: a whole 4x8x8 slice. The times are simulated.
512 devices in a mesh: files: 128 (over y, z, core), rep: 4 (over x).
Axes of the slice: x: 4, y: 8, z: 8, core: 2. Of those that a mesh axis runs over, the one named last changes fastest.
Arguments:
- tile_id: int32 [2097152], P(('files', 'rep')), may hold values from 0 to 127, as said below
- pix_row: int32 [2097152], P(('files', 'rep')), may hold values from 0 to 31
- pix_col: int32 [2097152], P(('files', 'rep')), may hold values from 0 to 127
- point_value: bfloat16 [2097152], P(('files', 'rep')), may hold values from -6 to 6
Outputs:
- tile_sums: float32 [128, 32, 128], P('files', 'rep')
Inputs may be any that keep to these rules, and one draw needn't show every extreme that they name: `tile_id`: of the points of one device, at most 128 lie in tiles of one file group (tile id modulo 128), and on every device some group holds exactly 128 of them.
All inputs are finite; a program needn't handle non-finite values.
Results may differ from a plain program's by a relative error of at most 0.0003.
Values sent between devices are 32-bit elements; how exact they have to be, the bound alone decides.
A program may use at most 64 MiB of HBM per device.

v0:
```python
import jax
import jax.numpy as jnp
from jax import lax
from jax.sharding import Mesh
from jax.sharding import PartitionSpec as P

CW = 4096
TC = 128
TR = 32
BAND = 128
FILES = ("files_0", "files_1", "files_2")
FILES_REP = ("files_0", "files_1", "files_2", "rep")


def in_blocks(value, dim, size):
    lengths = value.shape
    tiles = value.reshape(*lengths[:dim], size, lengths[dim] // size, *lengths[dim + 1 :])
    return jnp.moveaxis(tiles, dim, 0)


def sent_and_summed(value, axis, dim):
    size = lax.axis_size(axis)
    tiles = lax.all_to_all(in_blocks(value, dim, size), axis, 0, 0, tiled=True)
    return jnp.sum(tiles, axis=0)


def summed_rows(value, axes, dim):
    far, near = axes
    own = sent_and_summed(in_blocks(value, dim, lax.axis_size(far)), near, dim + 1)
    return jnp.sum(lax.all_to_all(own, far, 0, 0, tiled=True), axis=0)


def rasterize(dest_rows, dest_cols, point_vals, row_count, block_size):
    slot_total = dest_rows.shape[0]
    block_size = min(block_size, slot_total)
    block_count = slot_total // block_size
    row_ids = jnp.arange(row_count, dtype=jnp.int32)
    col_ids = jnp.arange(TC, dtype=jnp.int32)

    def accumulate(block_index, running):
        block_rows = lax.dynamic_slice_in_dim(dest_rows, block_index * block_size, block_size)
        block_cols = lax.dynamic_slice_in_dim(dest_cols, block_index * block_size, block_size)
        block_vals = lax.dynamic_slice_in_dim(point_vals, block_index * block_size, block_size)
        row_onehot = (block_rows[:, None] == row_ids[None, :]).astype(jnp.bfloat16)
        spread = jnp.where(
            block_cols[:, None] == col_ids[None, :],
            block_vals[:, None],
            jnp.zeros((), jnp.bfloat16),
        )
        return running + lax.dot_general(
            row_onehot, spread, (((0,), (0,)), ((), ())), preferred_element_type=jnp.float32
        )

    return lax.fori_loop(0, block_count, accumulate, jnp.zeros((row_count, TC), jnp.float32))


def per_device(tile_id, pix_row, pix_col, point_value):
    file_groups = lax.axis_size(FILES)
    rep_groups = lax.axis_size("rep")
    tile_count = BAND // TR * (CW // TC)
    owned = tile_count // file_groups
    quarter = TR // rep_groups
    tile_owner = tile_id % file_groups
    tile_local = tile_id // file_groups
    row_group = pix_row // quarter
    row_inner = pix_row % quarter
    target = ((row_group * file_groups + tile_owner) * owned + tile_local) * quarter + row_inner
    by_rep = sent_and_summed(
        rasterize(
            target, pix_col, point_value, file_groups * owned * quarter * lax.axis_size("rep"), 512
        ),
        "rep",
        0,
    )
    result = summed_rows(by_rep, (("files_0", "files_1"), "files_2"), 0)
    return result.reshape(owned, quarter, TC)


def solution(mesh):
    split = Mesh(
        mesh.devices.reshape(8, 8, 2, mesh.shape["rep"]), ("files_0", "files_1", "files_2", "rep")
    )
    return jax.shard_map(
        per_device,
        mesh=split,
        in_specs=(P(FILES_REP), P(FILES_REP), P(FILES_REP), P(FILES_REP)),
        out_specs=P(FILES, "rep", None),
        check_vma=False,
    )
```

profile of v0, /device:TPU:1, one launch (start us, length us, event | category | flops | bytes accessed | tf_op | source)
XLA Modules:
  0.0 108.9 jit_solution(8511333265872563695)
XLA Ops:
  0.0 0.8 fusion.17
  0.8 40.8 %while.14 = (s32[]{:T(128)}, f32[4096,128]{1,0:T(8,128)S(1)}, s32[4096]{0:T(1024)S(1)}, s32[4096]{0:T(1024)}, bf16[4096]{0:T(1024)(128)(2,1)}, /*index=5*/s32[]{:T(128)}, s32[]{:T(128)}, s32[]{:T(128)}, s32[]{:T(128)}) while((s32[]{:T(128)}, f32[4096,128]{1,0:T(8,128)S(1)}, s32[4096]{0:T(1024)S(1)}, s32[4096]{0:T(1024)}, ...), condition=%wide.region_1.2_spmd.clone, body=%wide.region_0.1_spmd.clone.sunk | while | flops 540147712 | bytes 4209833 | solution.py:54
  0.8 0.8 dynamic_slice.29
  1.6 0.8 dynamic_slice.28
  2.3 0.1 dynamic_slice.27
  2.4 3.5 %fusion.29 = f32[4096,128]{1,0:T(8,128)S(1)} fusion(s32[512]{0:T(512)S(1)} %dynamic_slice.27, f32[4096,128]{1,0:T(8,128)S(1)} %get-tuple-element.203, pred[]{:T(512)S(6)} %compare.9, s32[512]{0:T(512)S(1)} %dynamic_slice.28, bf16[512]{0:T(512)(128)(2,1)S(1)} %dynamic_slice.29), kind=kOutput, calls=%fused_computation.4.clone.1 | convolution fusion | flops 540147712 | bytes 4199425 | tf_op jit(solution)/shard_map/while/body/eval_jaxpr/dot_general | solution.py:50
  5.9 0.8 dynamic_slice.29
  6.7 0.8 dynamic_slice.28
  7.4 0.1 dynamic_slice.27
  7.5 3.5 %fusion.29 = f32[4096,128]{1,0:T(8,128)S(1)} fusion(s32[512]{0:T(512)S(1)} %dynamic_slice.27, f32[4096,128]{1,0:T(8,128)S(1)} %get-tuple-element.203, pred[]{:T(512)S(6)} %compare.9, s32[512]{0:T(512)S(1)} %dynamic_slice.28, bf16[512]{0:T(512)(128)(2,1)S(1)} %dynamic_slice.29), kind=kOutput, calls=%fused_computation.4.clone.1 | convolution fusion | flops 540147712 | bytes 4199425 | tf_op jit(solution)/shard_map/while/body/eval_jaxpr/dot_general | solution.py:50
  11.0 0.8 dynamic_slice.29
  11.8 0.8 dynamic_slice.28
  12.5 0.1 dynamic_slice.27
  12.6 3.5 %fusion.29 = f32[4096,128]{1,0:T(8,128)S(1)} fusion(s32[512]{0:T(512)S(1)} %dynamic_slice.27, f32[4096,128]{1,0:T(8,128)S(1)} %get-tuple-element.203, pred[]{:T(512)S(6)} %compare.9, s32[512]{0:T(512)S(1)} %dynamic_slice.28, bf16[512]{0:T(512)(128)(2,1)S(1)} %dynamic_slice.29), kind=kOutput, calls=%fused_computation.4.clone.1 | convolution fusion | flops 540147712 | bytes 4199425 | tf_op jit(solution)/shard_map/while/body/eval_jaxpr/dot_general | solution.py:50
  16.1 0.8 dynamic_slice.29
  16.9 0.8 dynamic_slice.28
  17.6 0.1 dynamic_slice.27
  17.7 3.5 %fusion.29 = f32[4096,128]{1,0:T(8,128)S(1)} fusion(s32[512]{0:T(512)S(1)} %dynamic_slice.27, f32[4096,128]{1,0:T(8,128)S(1)} %get-tuple-element.203, pred[]{:T(512)S(6)} %compare.9, s32[512]{0:T(512)S(1)} %dynamic_slice.28, bf16[512]{0:T(512)(128)(2,1)S(1)} %dynamic_slice.29), kind=kOutput, calls=%fused_computation.4.clone.1 | convolution fusion | flops 540147712 | bytes 4199425 | tf_op jit(solution)/shard_map/while/body/eval_jaxpr/dot_general | solution.py:50
  21.2 0.8 dynamic_slice.29
  22.0 0.8 dynamic_slice.28
  22.7 0.1 dynamic_slice.27
  22.8 3.5 %fusion.29 = f32[4096,128]{1,0:T(8,128)S(1)} fusion(s32[512]{0:T(512)S(1)} %dynamic_slice.27, f32[4096,128]{1,0:T(8,128)S(1)} %get-tuple-element.203, pred[]{:T(512)S(6)} %compare.9, s32[512]{0:T(512)S(1)} %dynamic_slice.28, bf16[512]{0:T(512)(128)(2,1)S(1)} %dynamic_slice.29), kind=kOutput, calls=%fused_computation.4.clone.1 | convolution fusion | flops 540147712 | bytes 4199425 | tf_op jit(solution)/shard_map/while/body/eval_jaxpr/dot_general | solution.py:50
  26.3 0.8 dynamic_slice.29
  27.1 0.8 dynamic_slice.28
  27.8 0.1 dynamic_slice.27
  27.9 3.5 %fusion.29 = f32[4096,128]{1,0:T(8,128)S(1)} fusion(s32[512]{0:T(512)S(1)} %dynamic_slice.27, f32[4096,128]{1,0:T(8,128)S(1)} %get-tuple-element.203, pred[]{:T(512)S(6)} %compare.9, s32[512]{0:T(512)S(1)} %dynamic_slice.28, bf16[512]{0:T(512)(128)(2,1)S(1)} %dynamic_slice.29), kind=kOutput, calls=%fused_computation.4.clone.1 | convolution fusion | flops 540147712 | bytes 4199425 | tf_op jit(solution)/shard_map/while/body/eval_jaxpr/dot_general | solution.py:50
  31.4 0.8 dynamic_slice.29
  32.2 0.8 dynamic_slice.28
  32.9 0.1 dynamic_slice.27
  33.0 3.5 %fusion.29 = f32[4096,128]{1,0:T(8,128)S(1)} fusion(s32[512]{0:T(512)S(1)} %dynamic_slice.27, f32[4096,128]{1,0:T(8,128)S(1)} %get-tuple-element.203, pred[]{:T(512)S(6)} %compare.9, s32[512]{0:T(512)S(1)} %dynamic_slice.28, bf16[512]{0:T(512)(128)(2,1)S(1)} %dynamic_slice.29), kind=kOutput, calls=%fused_computation.4.clone.1 | convolution fusion | flops 540147712 | bytes 4199425 | tf_op jit(solution)/shard_map/while/body/eval_jaxpr/dot_general | solution.py:50
  36.5 0.8 dynamic_slice.29
  37.3 0.8 dynamic_slice.28
  38.0 0.1 dynamic_slice.27
  38.1 3.5 %fusion.29 = f32[4096,128]{1,0:T(8,128)S(1)} fusion(s32[512]{0:T(512)S(1)} %dynamic_slice.27, f32[4096,128]{1,0:T(8,128)S(1)} %get-tuple-element.203, pred[]{:T(512)S(6)} %compare.9, s32[512]{0:T(512)S(1)} %dynamic_slice.28, bf16[512]{0:T(512)(128)(2,1)S(1)} %dynamic_slice.29), kind=kOutput, calls=%fused_computation.4.clone.1 | convolution fusion | flops 540147712 | bytes 4199425 | tf_op jit(solution)/shard_map/while/body/eval_jaxpr/dot_general | solution.py:50
  41.6 0.0 copy-start
  41.6 1.3 %copy-done = f32[4096,128]{1,0:T(8,128)} copy-done((f32[4096,128]{1,0:T(8,128)}, f32[4096,128]{1,0:T(8,128)S(1)}, u32[]{:S(2)}) %copy-start) | copy-done | bytes 2097176
  42.9 25.4 %all_to_all.15 = f32[4,1024,128]{2,1,0:T(8,128)S(1)} all-to-all(f32[4,1024,128]{2,1,0:T(8,128)} %bitcast.5), channel_id=1, replica_groups=mesh['files_0'=8,'files_1'=8,'files_2'=2,'rep'=4] {'rep'}, dimensions={0} | all-to-all | bytes 4194304 | tf_op jit(solution)/shard_map/all_to_all | solution.py:23
  68.3 0.1 reduce_sum.27
  68.5 10.5 %all_to_all.16 = f32[2,64,8,128]{3,2,1,0:T(8,128)S(1)} all-to-all(f32[2,64,8,128]{3,2,1,0:T(8,128)S(1)} %copy.6), channel_id=1, replica_groups=mesh['files_0'=8,'files_1'=8,'files_2'=2,'rep'=4] {'files_2'}, dimensions={0} | all-to-all | bytes 1048576 | tf_op jit(solution)/shard_map/all_to_all | solution.py:23
  79.1 29.2 %all_to_all.17 = f32[64,8,128]{2,1,0:T(8,128)S(1)} all-to-all(f32[64,8,128]{2,1,0:T(8,128)S(1)} %reduce_sum.28), channel_id=1, replica_groups=mesh['files_0'=8,'files_1'=8,'files_2'=2,'rep'=4] {'files_0','files_1'}, dimensions={0} | all-to-all | bytes 524288 | tf_op jit(solution)/shard_map/all_to_all | solution.py:30
  108.3 0.7 reduce_sum.29
  (3 shorter events, 0.1 us)
Async XLA Ops:
  41.6 1.4 %copy-start = (f32[4096,128]{1,0:T(8,128)}, f32[4096,128]{1,0:T(8,128)S(1)}, u32[]{:S(2)}) copy-start(f32[4096,128]{1,0:T(8,128)S(1)} %get-tuple-element.129) | copy-start | bytes 6291460
where the time goes:
time: 110 us; the launch traced here: 109 us
  blocking collectives  65.1 us (59%)
  matrix products  27.8 us (25%)
  local copies, waits for them, and re-layouts  14.1 us (13%)
  other arithmetic  1.61 us (1%)
    all_to_all x2, blocking collectives, sent_and_summed(): tiles = lax.all_to_all(in_blocks(value, dim, size), axis, 0, 0, tiled=True)  35.9 us
    all_to_all x1, blocking collectives, summed_rows(): return jnp.sum(lax.all_to_all(own, far, 0, 0, tiled=True), axis=0)  29.2 us
    dot_general x8, matrix products, accumulate(): lax.dot_general(row_onehot, spread, (((0,), (0,)), ((), ())), preferred_e...  27.8 us
    dynamic_slice x8, local copies, waits for them, and re-layouts, accumulate(): lax.dynamic_slice_in_dim(point_vals, block_index * block_size, block_size)  6.08 us
    dynamic_slice x8, local copies, waits for them, and re-layouts, accumulate(): lax.dynamic_slice_in_dim(dest_cols, block_index * block_size, block_size)  6.07 us

commit v1 on v0

v1 whole, which is shorter than its diff:
```python
import functools

import jax
import jax.numpy as jnp
from jax import lax
from jax.experimental import pallas as pl
from jax.experimental.pallas import tpu as pltpu
from jax.sharding import PartitionSpec as P

TC = 128
TR = 32
CAP = 128
LANES = 128
SUB = 16
MESH = pl.DeviceIdType.MESH
BF = jnp.bfloat16
F32 = jnp.float32
NT = (((1,), (1,)), ((), ()))


def packed_row(row):
    return jnp.broadcast_to(row, (SUB, LANES)).astype(BF)


def packed_iota(rows):
    count = lax.broadcasted_iota(jnp.int32, (rows // SUB, SUB, LANES), 0) * SUB
    return (count + lax.broadcasted_iota(jnp.int32, (rows // SUB, SUB, LANES), 1)).astype(F32).astype(BF)


def kernel(
    files,
    reps,
    tid_hbm,
    row_hbm,
    col_hbm,
    val_hbm,
    out_ref,
    tid_in,
    row_in,
    col_in,
    val_in,
    points,
    send,
    recv,
    part,
    gathered,
    in_sem,
    send_sem,
    recv_sem,
    part_send_sem,
    part_recv_sem,
):
    f = lax.axis_index("files")
    r = lax.axis_index("rep")
    blocks = tid_in.shape[0]
    quarter = TR // reps

    loads = [
        pltpu.make_async_copy(source, target, in_sem.at[i])
        for i, (source, target) in enumerate(
            ((tid_hbm, tid_in), (row_hbm, row_in), (col_hbm, col_in), (val_hbm, val_in))
        )
    ]
    for load in loads:
        load.start()

    barrier = pltpu.get_barrier_semaphore()

    def greet(k, _):
        peer = lax.rem(f + k, files)
        pl.semaphore_signal(barrier, inc=1, device_id={"files": peer, "rep": r}, device_id_type=MESH)
        return 0

    lax.fori_loop(1, files, greet, 0)
    for k in range(1, reps):
        pl.semaphore_signal(
            barrier, inc=1, device_id={"files": f, "rep": lax.rem(r + k, reps)}, device_id_type=MESH
        )

    for load in loads:
        load.wait()
    points[0] = tid_in[...].astype(F32)
    points[1] = row_in[...].astype(F32)
    points[2] = col_in[...].astype(F32)
    points[3] = val_in[...].astype(F32)

    iota = packed_iota(LANES)
    one, zero = jnp.ones((), BF), jnp.zeros((), BF)

    def tally(b, total):
        tid = packed_row(points[0, pl.ds(b, 1), :])
        return total + jnp.where(iota == tid[None], one, zero)

    total = lax.fori_loop(0, blocks, tally, jnp.zeros((LANES // SUB, SUB, LANES), BF), unroll=8)
    earlier = jnp.where(
        lax.broadcasted_iota(jnp.int32, (LANES, LANES), 0) < lax.broadcasted_iota(jnp.int32, (LANES, LANES), 1),
        1.0,
        0.0,
    ).astype(BF)
    before = jnp.dot(total.reshape(LANES, LANES), earlier, preferred_element_type=F32)
    before = before.astype(BF).reshape(LANES // SUB, SUB, LANES)

    def place(b, carry):
        before, packed = carry
        lefts, rights = [], []
        for half in range(2):
            at = b * 2 + half
            hit = iota == packed_row(points[0, pl.ds(at, 1), :])[None]
            slot = jnp.sum(jnp.where(hit, before, zero), axis=0)
            slot = jnp.sum(slot.astype(F32), axis=0, keepdims=True)
            before = before + jnp.where(hit, one, zero)
            rights.append(jnp.where(iota == packed_row(slot)[None], one, zero).reshape(LANES, LANES))
            lefts.append(
                jnp.concatenate(
                    [
                        jnp.where(hit, packed_row(points[i, pl.ds(at, 1), :])[None], zero).reshape(LANES, LANES)
                        for i in (1, 2, 3)
                    ],
                    axis=0,
                )
            )
        left, right = jnp.concatenate(lefts, axis=1), jnp.concatenate(rights, axis=1)
        return before, packed + lax.dot_general(left, right, NT, preferred_element_type=F32)

    _, packed = lax.fori_loop(
        0, blocks // 2, place, (before, jnp.zeros((3 * LANES, CAP), F32)), unroll=4
    )
    send[:, 0, :] = packed[2 * LANES :][:files]
    send[:, 1, :] = (packed[:LANES] * TC + packed[LANES : 2 * LANES])[:files]

    pl.semaphore_wait(barrier, files - 1 + reps - 1)

    def scatter(k, _):
        peer = lax.rem(f + k, files)
        pltpu.make_async_remote_copy(
            src_ref=send.at[peer],
            dst_ref=recv.at[k],
            send_sem=send_sem,
            recv_sem=recv_sem,
            device_id={"files": peer, "rep": r},
            device_id_type=MESH,
        ).start()
        return 0

    lax.fori_loop(1, files, scatter, 0)
    recv[0] = send[f]
    whole = recv.at[pl.ds(1, files - 1)]
    pltpu.make_async_copy(whole, whole, recv_sem).wait()

    row_iota = packed_iota(TR)

    def raster(s, total):
        lefts, rights = [], []
        for half in range(8):
            block = recv[s * 8 + half]
            cell = block[1:2]
            row = jnp.floor(cell * (1.0 / TC))
            col = cell - row * TC
            rights.append(jnp.where(row_iota == packed_row(row)[None], one, zero).reshape(TR, LANES))
            lefts.append(
                jnp.where(iota == packed_row(col)[None], packed_row(block[0:1])[None], zero).reshape(LANES, LANES)
            )
        left, right = jnp.concatenate(lefts, axis=1), jnp.concatenate(rights, axis=1)
        return total + lax.dot_general(left, right, NT, preferred_element_type=F32)

    tile = lax.fori_loop(0, files // 8, raster, jnp.zeros((TC, TR), F32), unroll=2 if files % 16 == 0 else 1)
    part[...] = tile.T.reshape(reps, quarter, TC)

    for k in range(1, reps):
        peer = lax.rem(r + k, reps)
        pltpu.make_async_remote_copy(
            src_ref=part.at[peer],
            dst_ref=gathered.at[k - 1],
            send_sem=part_send_sem,
            recv_sem=part_recv_sem,
            device_id={"files": f, "rep": peer},
            device_id_type=MESH,
        ).start()
    pltpu.make_async_copy(gathered, gathered, part_recv_sem).wait()
    out = part[r]
    for k in range(reps - 1):
        out = out + gathered[k]
    out_ref[...] = out

    sent = send.at[pl.ds(1, files - 1)]
    pltpu.make_async_copy(sent, sent, send_sem).wait()
    pltpu.make_async_copy(gathered, gathered, part_send_sem).wait()


def solution(mesh):
    files, reps = mesh.shape["files"], mesh.shape["rep"]

    def per_device(tile_id, pix_row, pix_col, point_value):
        count = tile_id.shape[0]
        blocks = count // LANES
        shaped = [a.reshape(blocks, LANES) for a in (tile_id, pix_row, pix_col, point_value)]
        out = pl.pallas_call(
            functools.partial(kernel, files, reps),
            out_shape=jax.ShapeDtypeStruct((TR // reps, TC), F32),
            in_specs=[pl.BlockSpec(memory_space=pl.ANY)] * 4,
            out_specs=pl.BlockSpec(memory_space=pltpu.VMEM),
            scratch_shapes=[
                pltpu.VMEM((blocks, LANES), jnp.int32),
                pltpu.VMEM((blocks, LANES), jnp.int32),
                pltpu.VMEM((blocks, LANES), jnp.int32),
                pltpu.VMEM((blocks, LANES), BF),
                pltpu.VMEM((4, blocks, LANES), F32),
                pltpu.VMEM((files, 2, CAP), F32),
                pltpu.VMEM((files, 2, CAP), F32),
                pltpu.VMEM((reps, TR // reps, TC), F32),
                pltpu.VMEM((reps - 1, TR // reps, TC), F32),
                pltpu.SemaphoreType.DMA((4,)),
                pltpu.SemaphoreType.DMA,
                pltpu.SemaphoreType.DMA,
                pltpu.SemaphoreType.DMA,
                pltpu.SemaphoreType.DMA,
            ],
            compiler_params=pltpu.CompilerParams(collective_id=0, has_side_effects=True),
        )(*shaped)
        return out[None]

    spec = P(("files", "rep"))
    return jax.shard_map(
        per_device,
        mesh=mesh,
        in_specs=(spec, spec, spec, spec),
        out_specs=P("files", "rep", None),
        check_vma=False,
    )
```

time: 110 us -> 32.8 us (0.30)
  blocking collectives: 65.1 us -> 0 us
  Pallas kernels: 0 us -> 31.4 us
  matrix products: 27.8 us -> 0 us
  local copies, waits for them, and re-layouts: 14.1 us -> 1.28 us
  other arithmetic: 1.61 us -> 0 us
    all_to_all x3 -> x0, blocking collectives: 65.1 us -> none  [the longest x2 35.9 us: sent_and_summed(): tiles = lax.all_to_all(in_blocks(value, dim, size), axis, 0, 0, tiled=True)]
    pallas_call x0 -> x1, Pallas kernels: none -> 31.4 us  [per_device(): pl.pallas_call(functools.partial(kernel, files, reps), out_shape=jax.Shap...]
    dot_general x8 -> x0, matrix products: 27.8 us -> none  [accumulate(): lax.dot_general(row_onehot, spread, (((0,), (0,)), ((), ())), preferred_e...]
    dynamic_slice x24 -> x0, local copies, waits for them, and re-layouts: 12.7 us -> none  [the longest x8 6.08 us: accumulate(): lax.dynamic_slice_in_dim(point_vals, block_index * block_size, block_size)]
where the time goes in v1:
time: 32.8 us; the launch traced here: 32.7 us
  Pallas kernels  31.4 us (96%)
  local copies, waits for them, and re-layouts  1.28 us (4%)
    pallas_call x1, Pallas kernels, per_device(): pl.pallas_call(functools.partial(kernel, files, reps), out_shape=jax.Shap...  31.4 us
    unnamed x1, local copies, waits for them, and re-layouts  1.28 us

profile of v1, /device:TPU:1, one launch (start us, length us, event | category | flops | bytes accessed | tf_op | source)
XLA Modules:
  0.0 32.7 jit_solution(3505258228798927764)
XLA Ops:
  0.0 31.4 %shard_map.46 = f32[8,128]{1,0:T(8,128)} custom-call(s32[32,128]{1,0:T(8,128)} %bitcast.5, s32[32,128]{1,0:T(8,128)} %bitcast.6, s32[32,128]{1,0:T(8,128)} %bitcast.7, bf16[32,128]{1,0:T(8,128)(2,1)} %bitcast.9), custom_call_target="tpu_custom_call" | custom-call | tf_op jit(solution)/shard_map/pallas_call | solution.py:197
  31.4 1.3 %copy.6 = f32[1,8,128]{2,1,0:T(8,128)} copy(f32[1,8,128]{2,1,0:T(8,128)} %bitcast.8) | data formatting | bytes 8192

commit v2 on v1

--- a/solution.py
+++ b/solution.py
@@ -12,6 +12,8 @@
 CAP = 128
 LANES = 128
 SUB = 16
+DEPTH = 8
+RASTER = 8
 MESH = pl.DeviceIdType.MESH
 BF = jnp.bfloat16
 F32 = jnp.float32
@@ -47,11 +49,19 @@
     in_sem,
     send_sem,
     recv_sem,
+    above,
     part_send_sem,
     part_recv_sem,
 ):
     f = lax.axis_index("files")
     r = lax.axis_index("rep")
+    depth, line = recv.shape[:2]
+    z = lax.rem(f // 2, depth)
+    i = f // (2 * depth) * 2 + lax.rem(f, 2)
+
+    def file_at(place, level):
+        return (place // 2 * depth + level) * 2 + lax.rem(place, 2)
+
     blocks = tid_in.shape[0]
     quarter = TR // reps
 
@@ -65,13 +75,11 @@
         load.start()
 
     barrier = pltpu.get_barrier_semaphore()
-
-    def greet(k, _):
-        peer = lax.rem(f + k, files)
-        pl.semaphore_signal(barrier, inc=1, device_id={"files": peer, "rep": r}, device_id_type=MESH)
-        return 0
-
-    lax.fori_loop(1, files, greet, 0)
+    for j in range(1, line):
+        peer = lax.rem(i + j, line)
+        pl.semaphore_signal(
+            barrier, inc=1, device_id={"files": file_at(peer, z), "rep": r}, device_id_type=MESH
+        )
     for k in range(1, reps):
         pl.semaphore_signal(
             barrier, inc=1, device_id={"files": f, "rep": lax.rem(r + k, reps)}, device_id_type=MESH
@@ -128,42 +136,74 @@
     send[:, 0, :] = packed[2 * LANES :][:files]
     send[:, 1, :] = (packed[:LANES] * TC + packed[LANES : 2 * LANES])[:files]
 
-    pl.semaphore_wait(barrier, files - 1 + reps - 1)
-
-    def scatter(k, _):
-        peer = lax.rem(f + k, files)
-        pltpu.make_async_remote_copy(
-            src_ref=send.at[peer],
-            dst_ref=recv.at[k],
-            send_sem=send_sem,
-            recv_sem=recv_sem,
-            device_id={"files": peer, "rep": r},
-            device_id_type=MESH,
-        ).start()
+    own = pltpu.make_async_copy(send.at[f], recv.at[z, i], recv_sem.at[z])
+    own.start()
+
+    def scatter(level, first):
+        def one_peer(j, _):
+            peer = file_at(lax.rem(i + j, line), level)
+            pltpu.make_async_remote_copy(
+                src_ref=send.at[peer],
+                dst_ref=recv.at[z, i],
+                send_sem=send_sem,
+                recv_sem=recv_sem.at[z],
+                device_id={"files": peer, "rep": r},
+                device_id_type=MESH,
+            ).start()
+            return 0
+
+        lax.fori_loop(first, line, one_peer, 0)
+
+    pl.semaphore_wait(barrier, line - 1 + reps - 1 + jnp.minimum(z, 1))
+
+    @pl.when(z < depth - 1)
+    def _():
+        pl.semaphore_signal(
+            barrier, inc=1, device_id={"files": file_at(i, z + 1), "rep": r}, device_id_type=MESH
+        )
+
+    def lower(level, _):
+        scatter(level, 0)
         return 0
 
-    lax.fori_loop(1, files, scatter, 0)
-    recv[0] = send[f]
-    whole = recv.at[pl.ds(1, files - 1)]
-    pltpu.make_async_copy(whole, whole, recv_sem).wait()
+    def announce(level, _):
+        pl.semaphore_signal(
+            above.at[z], inc=1, device_id={"files": file_at(i, level), "rep": r}, device_id_type=MESH
+        )
+        return 0
+
+    lax.fori_loop(0, z, announce, 0)
+    lax.fori_loop(0, z, lower, 0)
+    scatter(z, 1)
+
+    def upper(level, _):
+        pl.semaphore_wait(above.at[level], 1)
+        scatter(level, 0)
+        return 0
+
+    lax.fori_loop(z + 1, depth, upper, 0)
 
     row_iota = packed_iota(TR)
 
-    def raster(s, total):
-        lefts, rights = [], []
-        for half in range(8):
-            block = recv[s * 8 + half]
-            cell = block[1:2]
-            row = jnp.floor(cell * (1.0 / TC))
-            col = cell - row * TC
-            rights.append(jnp.where(row_iota == packed_row(row)[None], one, zero).reshape(TR, LANES))
-            lefts.append(
-                jnp.where(iota == packed_row(col)[None], packed_row(block[0:1])[None], zero).reshape(LANES, LANES)
-            )
-        left, right = jnp.concatenate(lefts, axis=1), jnp.concatenate(rights, axis=1)
-        return total + lax.dot_general(left, right, NT, preferred_element_type=F32)
-
-    tile = lax.fori_loop(0, files // 8, raster, jnp.zeros((TC, TR), F32), unroll=2 if files % 16 == 0 else 1)
+    def raster(level, total):
+        landed = recv.at[level]
+        pltpu.make_async_copy(landed, landed, recv_sem.at[level]).wait()
+        for group in range(0, line, RASTER):
+            lefts, rights = [], []
+            for source in range(group, min(group + RASTER, line)):
+                block = recv[level, source]
+                cell = block[1:2]
+                row = jnp.floor(cell * (1.0 / TC))
+                col = cell - row * TC
+                rights.append(jnp.where(row_iota == packed_row(row)[None], one, zero).reshape(TR, LANES))
+                lefts.append(
+                    jnp.where(iota == packed_row(col)[None], packed_row(block[0:1])[None], zero).reshape(LANES, LANES)
+                )
+            left, right = jnp.concatenate(lefts, axis=1), jnp.concatenate(rights, axis=1)
+            total = total + lax.dot_general(left, right, NT, preferred_element_type=F32)
+        return total
+
+    tile = lax.fori_loop(0, depth, raster, jnp.zeros((TC, TR), F32))
     part[...] = tile.T.reshape(reps, quarter, TC)
 
     for k in range(1, reps):
@@ -182,13 +222,14 @@
         out = out + gathered[k]
     out_ref[...] = out
 
-    sent = send.at[pl.ds(1, files - 1)]
+    sent = send.at[pl.ds(0, files - 1)]
     pltpu.make_async_copy(sent, sent, send_sem).wait()
     pltpu.make_async_copy(gathered, gathered, part_send_sem).wait()
 
 
 def solution(mesh):
     files, reps = mesh.shape["files"], mesh.shape["rep"]
+    depth = DEPTH if files % (2 * DEPTH) == 0 else 2
 
     def per_device(tile_id, pix_row, pix_col, point_value):
         count = tile_id.shape[0]
@@ -206,12 +247,13 @@
                 pltpu.VMEM((blocks, LANES), BF),
                 pltpu.VMEM((4, blocks, LANES), F32),
                 pltpu.VMEM((files, 2, CAP), F32),
-                pltpu.VMEM((files, 2, CAP), F32),
+                pltpu.VMEM((depth, files // depth, 2, CAP), F32),
                 pltpu.VMEM((reps, TR // reps, TC), F32),
                 pltpu.VMEM((reps - 1, TR // reps, TC), F32),
                 pltpu.SemaphoreType.DMA((4,)),
                 pltpu.SemaphoreType.DMA,
-                pltpu.SemaphoreType.DMA,
+                pltpu.SemaphoreType.DMA((depth,)),
+                pltpu.SemaphoreType.REGULAR((depth,)),
                 pltpu.SemaphoreType.DMA,
                 pltpu.SemaphoreType.DMA,
             ],

time: 32.8 us -> 28.8 us (0.88)
  Pallas kernels: 31.4 us -> 27.3 us
    pallas_call x1, Pallas kernels: 31.4 us -> 27.3 us  [per_device(): pl.pallas_call(functools.partial(kernel, files, reps), out_shape=jax.Shap...]
where the time goes in v2:
time: 28.8 us; the launch traced here: 28.5 us
  Pallas kernels  27.3 us (95%)
  local copies, waits for them, and re-layouts  1.28 us (4%)
    pallas_call x1, Pallas kernels, per_device(): pl.pallas_call(functools.partial(kernel, files, reps), out_shape=jax.Shap...  27.3 us
    unnamed x1, local copies, waits for them, and re-layouts  1.28 us

profile of v2, /device:TPU:1, one launch (start us, length us, event | category | flops | bytes accessed | tf_op | source)
XLA Modules:
  0.0 28.5 jit_solution(2100819455609759824)
XLA Ops:
  0.0 27.3 %shard_map.46 = f32[8,128]{1,0:T(8,128)} custom-call(s32[32,128]{1,0:T(8,128)} %bitcast.5, s32[32,128]{1,0:T(8,128)} %bitcast.6, s32[32,128]{1,0:T(8,128)} %bitcast.7, bf16[32,128]{1,0:T(8,128)(2,1)} %bitcast.9), custom_call_target="tpu_custom_call" | custom-call | tf_op jit(solution)/shard_map/pallas_call | solution.py:238
  27.3 1.3 %copy.6 = f32[1,8,128]{2,1,0:T(8,128)} copy(f32[1,8,128]{2,1,0:T(8,128)} %bitcast.8) | data formatting | bytes 8192

commit v3 on v2

--- a/solution.py
+++ b/solution.py
@@ -14,6 +14,8 @@
 SUB = 16
 DEPTH = 8
 RASTER = 8
+GROUP = 32
+VMEM = 8 << 20
 MESH = pl.DeviceIdType.MESH
 BF = jnp.bfloat16
 F32 = jnp.float32
@@ -37,9 +39,7 @@
     col_hbm,
     val_hbm,
     out_ref,
-    tid_in,
-    row_in,
-    col_in,
+    ids_in,
     val_in,
     points,
     send,
@@ -62,14 +62,14 @@
     def file_at(place, level):
         return (place // 2 * depth + level) * 2 + lax.rem(place, 2)
 
-    blocks = tid_in.shape[0]
+    blocks = val_in.shape[0]
     quarter = TR // reps
 
     loads = [
-        pltpu.make_async_copy(source, target, in_sem.at[i])
-        for i, (source, target) in enumerate(
-            ((tid_hbm, tid_in), (row_hbm, row_in), (col_hbm, col_in), (val_hbm, val_in))
-        )
+        pltpu.make_async_copy(tid_hbm, ids_in.at[0], in_sem.at[0]),
+        pltpu.make_async_copy(row_hbm, ids_in.at[1], in_sem.at[0]),
+        pltpu.make_async_copy(col_hbm, ids_in.at[2], in_sem.at[0]),
+        pltpu.make_async_copy(val_hbm, val_in, in_sem.at[1]),
     ]
     for load in loads:
         load.start()
@@ -85,12 +85,13 @@
             barrier, inc=1, device_id={"files": f, "rep": lax.rem(r + k, reps)}, device_id_type=MESH
         )
 
-    for load in loads:
-        load.wait()
-    points[0] = tid_in[...].astype(F32)
-    points[1] = row_in[...].astype(F32)
-    points[2] = col_in[...].astype(F32)
-    points[3] = val_in[...].astype(F32)
+    pltpu.make_async_copy(ids_in, ids_in, in_sem.at[0]).wait()
+    loads[3].wait()
+    row = ids_in[1]
+    power = jnp.left_shift(1, row & 15).astype(F32) * jnp.where(row >= 16, 65536.0, 1.0)
+    points[0] = ids_in[0].astype(F32)
+    points[1] = (ids_in[2] + TC).astype(F32) * power
+    points[2] = val_in[...].astype(F32)
 
     iota = packed_iota(LANES)
     one, zero = jnp.ones((), BF), jnp.zeros((), BF)
@@ -111,18 +112,20 @@
     def place(b, carry):
         before, packed = carry
         lefts, rights = [], []
-        for half in range(2):
-            at = b * 2 + half
+        for step in range(group):
+            at = b * group + step
             hit = iota == packed_row(points[0, pl.ds(at, 1), :])[None]
             slot = jnp.sum(jnp.where(hit, before, zero), axis=0)
             slot = jnp.sum(slot.astype(F32), axis=0, keepdims=True)
-            before = before + jnp.where(hit, one, zero)
-            rights.append(jnp.where(iota == packed_row(slot)[None], one, zero).reshape(LANES, LANES))
-            lefts.append(
+            count = jnp.where(hit, one, zero)
+            before = before + count
+            lefts.append(count.reshape(LANES, LANES))
+            here = iota == packed_row(slot)[None]
+            rights.append(
                 jnp.concatenate(
                     [
-                        jnp.where(hit, packed_row(points[i, pl.ds(at, 1), :])[None], zero).reshape(LANES, LANES)
-                        for i in (1, 2, 3)
+                        jnp.where(here, packed_row(points[plane, pl.ds(at, 1), :])[None], zero).reshape(CAP, LANES)
+                        for plane in (1, 2)
                     ],
                     axis=0,
                 )
@@ -130,29 +133,37 @@
         left, right = jnp.concatenate(lefts, axis=1), jnp.concatenate(rights, axis=1)
         return before, packed + lax.dot_general(left, right, NT, preferred_element_type=F32)
 
-    _, packed = lax.fori_loop(
-        0, blocks // 2, place, (before, jnp.zeros((3 * LANES, CAP), F32)), unroll=4
-    )
-    send[:, 0, :] = packed[2 * LANES :][:files]
-    send[:, 1, :] = (packed[:LANES] * TC + packed[LANES : 2 * LANES])[:files]
-
-    own = pltpu.make_async_copy(send.at[f], recv.at[z, i], recv_sem.at[z])
+    group = min(GROUP, blocks)
+    _, packed = lax.fori_loop(0, blocks // group, place, (before, jnp.zeros((LANES, 2 * CAP), F32)))
+    code, row = packed[:files, :CAP], jnp.zeros((files, CAP), F32)
+    for bit in (16, 8, 4, 2, 1):
+        high = code >= 128.0 * 2.0**bit
+        code = jnp.where(high, code * 2.0**-bit, code)
+        row = row + jnp.where(high, float(bit), 0.0)
+    send[pl.ds(0, files, stride=2), :] = packed[:files, CAP:]
+    send[pl.ds(1, files, stride=2), :] = row * TC + (code - TC)
+
+    own = pltpu.make_async_copy(send.at[pl.ds(2 * f, 2)], recv.at[z, i], recv_sem.at[z])
     own.start()
 
-    def scatter(level, first):
-        def one_peer(j, _):
-            peer = file_at(lax.rem(i + j, line), level)
-            pltpu.make_async_remote_copy(
-                src_ref=send.at[peer],
-                dst_ref=recv.at[z, i],
-                send_sem=send_sem,
-                recv_sem=recv_sem.at[z],
-                device_id={"files": peer, "rep": r},
-                device_id_type=MESH,
-            ).start()
-            return 0
-
-        lax.fori_loop(first, line, one_peer, 0)
+    def scatter(level, skip):
+        for place in range(line):
+            peer = place // 2 * depth * 2 + place % 2 + level * 2
+
+            def start(peer=peer):
+                pltpu.make_async_remote_copy(
+                    src_ref=send.at[pl.ds(2 * peer, 2)],
+                    dst_ref=recv.at[z, i],
+                    send_sem=send_sem,
+                    recv_sem=recv_sem.at[z],
+                    device_id={"files": peer, "rep": r},
+                    device_id_type=MESH,
+                ).start()
+
+            if skip:
+                pl.when(i != place)(start)
+            else:
+                start()
 
     pl.semaphore_wait(barrier, line - 1 + reps - 1 + jnp.minimum(z, 1))
 
@@ -163,7 +174,7 @@
         )
 
     def lower(level, _):
-        scatter(level, 0)
+        scatter(level, False)
         return 0
 
     def announce(level, _):
@@ -174,11 +185,11 @@
 
     lax.fori_loop(0, z, announce, 0)
     lax.fori_loop(0, z, lower, 0)
-    scatter(z, 1)
+    scatter(z, True)
 
     def upper(level, _):
         pl.semaphore_wait(above.at[level], 1)
-        scatter(level, 0)
+        scatter(level, False)
         return 0
 
     lax.fori_loop(z + 1, depth, upper, 0)
@@ -222,7 +233,7 @@
         out = out + gathered[k]
     out_ref[...] = out
 
-    sent = send.at[pl.ds(0, files - 1)]
+    sent = send.at[pl.ds(0, 2 * (files - 1))]
     pltpu.make_async_copy(sent, sent, send_sem).wait()
     pltpu.make_async_copy(gathered, gathered, part_send_sem).wait()
 
@@ -238,27 +249,27 @@
         out = pl.pallas_call(
             functools.partial(kernel, files, reps),
             out_shape=jax.ShapeDtypeStruct((TR // reps, TC), F32),
-            in_specs=[pl.BlockSpec(memory_space=pl.ANY)] * 4,
+            in_specs=[pl.BlockSpec(memory_space=pltpu.HBM)] * 4,
             out_specs=pl.BlockSpec(memory_space=pltpu.VMEM),
             scratch_shapes=[
-                pltpu.VMEM((blocks, LANES), jnp.int32),
-                pltpu.VMEM((blocks, LANES), jnp.int32),
-                pltpu.VMEM((blocks, LANES), jnp.int32),
+                pltpu.VMEM((3, blocks, LANES), jnp.int32),
                 pltpu.VMEM((blocks, LANES), BF),
-                pltpu.VMEM((4, blocks, LANES), F32),
-                pltpu.VMEM((files, 2, CAP), F32),
+                pltpu.VMEM((3, blocks, LANES), F32),
+                pltpu.VMEM((2 * files, CAP), F32),
                 pltpu.VMEM((depth, files // depth, 2, CAP), F32),
                 pltpu.VMEM((reps, TR // reps, TC), F32),
                 pltpu.VMEM((reps - 1, TR // reps, TC), F32),
-                pltpu.SemaphoreType.DMA((4,)),
+                pltpu.SemaphoreType.DMA((2,)),
                 pltpu.SemaphoreType.DMA,
                 pltpu.SemaphoreType.DMA((depth,)),
                 pltpu.SemaphoreType.REGULAR((depth,)),
                 pltpu.SemaphoreType.DMA,
                 pltpu.SemaphoreType.DMA,
             ],
-            compiler_params=pltpu.CompilerParams(collective_id=0, has_side_effects=True),
-        )(*shaped)
+            compiler_params=pltpu.CompilerParams(
+                collective_id=0, has_side_effects=True, vmem_limit_bytes=VMEM
+            ),
+        )(*[pltpu.with_memory_space_constraint(a, pltpu.HBM) for a in shaped])
         return out[None]
 
     spec = P(("files", "rep"))

time: 28.8 us -> 26.4 us (0.917)
  Pallas kernels: 27.3 us -> 25.6 us
  local copies, waits for them, and re-layouts: 1.28 us -> 0.6 us
    pallas_call x1, Pallas kernels: 27.3 us -> 25.6 us  [per_device(): pl.pallas_call(functools.partial(kernel, files, reps), out_shape=jax.Shap...]
    unnamed x1, local copies, waits for them, and re-layouts: 1.28 us -> 0.6 us
where the time goes in v3:
time: 26.4 us; the launch traced here: 26.3 us
  Pallas kernels  25.6 us (97%)
  local copies, waits for them, and re-layouts  0.6 us (2%)
    pallas_call x1, Pallas kernels, per_device(): pl.pallas_call(functools.partial(kernel, files, reps), out_shape=jax.Shap...  25.6 us
    unnamed x1, local copies, waits for them, and re-layouts  0.6 us

profile of v3, /device:TPU:1, one launch (start us, length us, event | category | flops | bytes accessed | tf_op | source)
XLA Modules:
  0.0 26.3 jit_solution(18226077084756068776)
XLA Ops:
  0.0 25.6 %shard_map.46 = f32[8,128]{1,0:T(8,128)S(1)} custom-call(s32[32,128]{1,0:T(8,128)} %bitcast.6, s32[32,128]{1,0:T(8,128)} %bitcast.7, s32[32,128]{1,0:T(8,128)} %bitcast.8, bf16[32,128]{1,0:T(8,128)(2,1)} %bitcast.9), custom_call_target="tpu_custom_call" | custom-call | tf_op jit(solution)/shard_map/pallas_call | solution.py:249
  25.7 0.6 %copy.6 = f32[1,8,128]{2,1,0:T(8,128)} copy(f32[1,8,128]{2,1,0:T(8,128)S(1)} %bitcast.5) | data formatting | bytes 8192

commit v4 on v3

--- a/solution.py
+++ b/solution.py
@@ -59,8 +59,8 @@
     z = lax.rem(f // 2, depth)
     i = f // (2 * depth) * 2 + lax.rem(f, 2)
 
-    def file_at(place, level):
-        return (place // 2 * depth + level) * 2 + lax.rem(place, 2)
+    def file_on(place, level):
+        return place // 2 * depth * 2 + place % 2 + level * 2
 
     blocks = val_in.shape[0]
     quarter = TR // reps
@@ -75,15 +75,22 @@
         load.start()
 
     barrier = pltpu.get_barrier_semaphore()
-    for j in range(1, line):
-        peer = lax.rem(i + j, line)
-        pl.semaphore_signal(
-            barrier, inc=1, device_id={"files": file_at(peer, z), "rep": r}, device_id_type=MESH
-        )
+    def tell(semaphore, peer):
+        pl.semaphore_signal(semaphore, inc=1, device_id={"files": peer, "rep": r}, device_id_type=MESH)
+
+    for place in range(line):
+        pl.when(i != place)(functools.partial(tell, barrier, file_on(place, z)))
     for k in range(1, reps):
         pl.semaphore_signal(
             barrier, inc=1, device_id={"files": f, "rep": lax.rem(r + k, reps)}, device_id_type=MESH
         )
+
+    def greet(level, _):
+        for place in range(line):
+            tell(barrier, file_on(place, level))
+        return 0
+
+    lax.fori_loop(z + 1, depth, greet, 0)
 
     pltpu.make_async_copy(ids_in, ids_in, in_sem.at[0]).wait()
     loads[3].wait()
@@ -148,7 +155,7 @@
 
     def scatter(level, skip):
         for place in range(line):
-            peer = place // 2 * depth * 2 + place % 2 + level * 2
+            peer = file_on(place, level)
 
             def start(peer=peer):
                 pltpu.make_async_remote_copy(
@@ -165,22 +172,14 @@
             else:
                 start()
 
-    pl.semaphore_wait(barrier, line - 1 + reps - 1 + jnp.minimum(z, 1))
-
-    @pl.when(z < depth - 1)
-    def _():
-        pl.semaphore_signal(
-            barrier, inc=1, device_id={"files": file_at(i, z + 1), "rep": r}, device_id_type=MESH
-        )
+    pl.semaphore_wait(barrier, line - 1 + reps - 1 + z * line)
 
     def lower(level, _):
         scatter(level, False)
         return 0
 
     def announce(level, _):
-        pl.semaphore_signal(
-            above.at[z], inc=1, device_id={"files": file_at(i, level), "rep": r}, device_id_type=MESH
-        )
+        tell(above.at[z], f + (level - z) * 2)
         return 0
 
     lax.fori_loop(0, z, announce, 0)
@@ -196,7 +195,8 @@
 
     row_iota = packed_iota(TR)
 
-    def raster(level, total):
+    def raster(step, total):
+        level = jnp.where(z < depth // 2, step, depth - 1 - step)
         landed = recv.at[level]
         pltpu.make_async_copy(landed, landed, recv_sem.at[level]).wait()
         for group in range(0, line, RASTER):
@@ -211,11 +211,11 @@
                     jnp.where(iota == packed_row(col)[None], packed_row(block[0:1])[None], zero).reshape(LANES, LANES)
                 )
             left, right = jnp.concatenate(lefts, axis=1), jnp.concatenate(rights, axis=1)
-            total = total + lax.dot_general(left, right, NT, preferred_element_type=F32)
+            total = total + lax.dot_general(right, left, NT, preferred_element_type=F32)
         return total
 
-    tile = lax.fori_loop(0, depth, raster, jnp.zeros((TC, TR), F32))
-    part[...] = tile.T.reshape(reps, quarter, TC)
+    tile = lax.fori_loop(0, depth, raster, jnp.zeros((TR, TC), F32))
+    part[...] = tile.reshape(reps, quarter, TC)
 
     for k in range(1, reps):
         peer = lax.rem(r + k, reps)

time: 26.4 us -> 26 us (0.985)
  Pallas kernels: 25.6 us -> 25.2 us
    pallas_call x1, Pallas kernels: 25.6 us -> 25.2 us  [per_device(): pl.pallas_call(functools.partial(kernel, files, reps), out_shape=jax.Shap...]
where the time goes in v4:
time: 26 us; the launch traced here: 25.8 us
  Pallas kernels  25.2 us (97%)
  local copies, waits for them, and re-layouts  0.6 us (2%)
    pallas_call x1, Pallas kernels, per_device(): pl.pallas_call(functools.partial(kernel, files, reps), out_shape=jax.Shap...  25.2 us
    unnamed x1, local copies, waits for them, and re-layouts  0.6 us

profile of v4, /device:TPU:1, one launch (start us, length us, event | category | flops | bytes accessed | tf_op | source)
XLA Modules:
  0.0 25.8 jit_solution(3710758289943475547)
XLA Ops:
  0.0 25.2 %shard_map.46 = f32[8,128]{1,0:T(8,128)S(1)} custom-call(s32[32,128]{1,0:T(8,128)} %bitcast.6, s32[32,128]{1,0:T(8,128)} %bitcast.7, s32[32,128]{1,0:T(8,128)} %bitcast.8, bf16[32,128]{1,0:T(8,128)(2,1)} %bitcast.9), custom_call_target="tpu_custom_call" | custom-call | tf_op jit(solution)/shard_map/pallas_call | solution.py:249
  25.2 0.6 %copy.6 = f32[1,8,128]{2,1,0:T(8,128)} copy(f32[1,8,128]{2,1,0:T(8,128)S(1)} %bitcast.5) | data formatting | bytes 8192

commit v5 on v4

--- a/solution.py
+++ b/solution.py
@@ -50,26 +50,27 @@
     send_sem,
     recv_sem,
     above,
-    part_send_sem,
     part_recv_sem,
 ):
     f = lax.axis_index("files")
     r = lax.axis_index("rep")
     depth, line = recv.shape[:2]
     z = lax.rem(f // 2, depth)
-    i = f // (2 * depth) * 2 + lax.rem(f, 2)
+    y, core = f // (2 * depth), lax.rem(f, 2)
+    i = y * 2 + core
 
     def file_on(place, level):
         return place // 2 * depth * 2 + place % 2 + level * 2
 
+    half = depth // 2
     blocks = val_in.shape[0]
     quarter = TR // reps
 
     loads = [
-        pltpu.make_async_copy(tid_hbm, ids_in.at[0], in_sem.at[0]),
-        pltpu.make_async_copy(row_hbm, ids_in.at[1], in_sem.at[0]),
-        pltpu.make_async_copy(col_hbm, ids_in.at[2], in_sem.at[0]),
-        pltpu.make_async_copy(val_hbm, val_in, in_sem.at[1]),
+        pltpu.make_async_copy(tid_hbm, ids_in.at[0], in_sem),
+        pltpu.make_async_copy(row_hbm, ids_in.at[1], in_sem),
+        pltpu.make_async_copy(col_hbm, ids_in.at[2], in_sem),
+        pltpu.make_async_copy(val_hbm, val_in, in_sem),
     ]
     for load in loads:
         load.start()
@@ -78,8 +79,13 @@
     def tell(semaphore, peer):
         pl.semaphore_signal(semaphore, inc=1, device_id={"files": peer, "rep": r}, device_id_type=MESH)
 
-    for place in range(line):
-        pl.when(i != place)(functools.partial(tell, barrier, file_on(place, z)))
+    tell(barrier, f + 1 - 2 * core)
+    rows = line // 2
+    for step in sorted(range(1, rows), key=lambda step: min(step, rows - step)):
+        there = y + step
+        there = jnp.where(there >= rows, there - rows, there) * (2 * depth) + z * 2
+        tell(barrier, there)
+        tell(barrier, there + 1)
     for k in range(1, reps):
         pl.semaphore_signal(
             barrier, inc=1, device_id={"files": f, "rep": lax.rem(r + k, reps)}, device_id_type=MESH
@@ -92,8 +98,9 @@
 
     lax.fori_loop(z + 1, depth, greet, 0)
 
-    pltpu.make_async_copy(ids_in, ids_in, in_sem.at[0]).wait()
-    loads[3].wait()
+    loaded = send.at[pl.ds(0, blocks * 7 // 2)]
+    pltpu.make_async_copy(loaded, loaded, in_sem).wait()
+
     row = ids_in[1]
     power = jnp.left_shift(1, row & 15).astype(F32) * jnp.where(row >= 16, 65536.0, 1.0)
     points[0] = ids_in[0].astype(F32)
@@ -107,7 +114,7 @@
         tid = packed_row(points[0, pl.ds(b, 1), :])
         return total + jnp.where(iota == tid[None], one, zero)
 
-    total = lax.fori_loop(0, blocks, tally, jnp.zeros((LANES // SUB, SUB, LANES), BF), unroll=8)
+    total = lax.fori_loop(0, blocks, tally, jnp.zeros((LANES // SUB, SUB, LANES), BF), unroll=min(32, blocks))
     earlier = jnp.where(
         lax.broadcasted_iota(jnp.int32, (LANES, LANES), 0) < lax.broadcasted_iota(jnp.int32, (LANES, LANES), 1),
         1.0,
@@ -150,7 +157,7 @@
     send[pl.ds(0, files, stride=2), :] = packed[:files, CAP:]
     send[pl.ds(1, files, stride=2), :] = row * TC + (code - TC)
 
-    own = pltpu.make_async_copy(send.at[pl.ds(2 * f, 2)], recv.at[z, i], recv_sem.at[z])
+    own = pltpu.make_async_copy(send.at[pl.ds(2 * f, 2)], recv.at[z, i], recv_sem.at[jnp.maximum(z - half + 1, 0)])
     own.start()
 
     def scatter(level, skip):
@@ -162,7 +169,7 @@
                     src_ref=send.at[pl.ds(2 * peer, 2)],
                     dst_ref=recv.at[z, i],
                     send_sem=send_sem,
-                    recv_sem=recv_sem.at[z],
+                    recv_sem=recv_sem.at[jnp.maximum(z - half + 1, 0)],
                     device_id={"files": peer, "rep": r},
                     device_id_type=MESH,
                 ).start()
@@ -179,26 +186,39 @@
         return 0
 
     def announce(level, _):
-        tell(above.at[z], f + (level - z) * 2)
+        tell(above.at[jnp.where(z < half, 0, 1 + jnp.maximum(z - half, 0) // 2)], f + (level - z) * 2)
         return 0
 
+    @pl.when(z > 0)
+    def _():
+        scatter(0, False)
+
     lax.fori_loop(0, z, announce, 0)
-    lax.fori_loop(0, z, lower, 0)
+    lax.fori_loop(1, z, lower, 0)
     scatter(z, True)
 
     def upper(level, _):
-        pl.semaphore_wait(above.at[level], 1)
         scatter(level, False)
         return 0
 
-    lax.fori_loop(z + 1, depth, upper, 0)
+    for group, (start, stop) in enumerate([(1, half)] + [(k, min(k + 2, depth)) for k in range(half, depth, 2)]):
+        base = jnp.maximum(z + 1, start)
+
+        def heard(group=group, stop=stop, base=base):
+            pl.semaphore_wait(above.at[group], stop - base)
+            lax.fori_loop(base, stop, upper, 0)
+
+        pl.when(base < stop)(heard)
 
     row_iota = packed_iota(TR)
 
     def raster(step, total):
-        level = jnp.where(z < depth // 2, step, depth - 1 - step)
-        landed = recv.at[level]
-        pltpu.make_async_copy(landed, landed, recv_sem.at[level]).wait()
+        level = jnp.where(z < half, step, depth - 1 - step)
+        landed, lower_half = recv.at[level], recv.at[pl.ds(0, half)]
+        alone = pltpu.make_async_copy(landed, landed, recv_sem.at[jnp.maximum(level - half + 1, 0)])
+        pl.when(level >= half)(alone.wait)
+        together = pltpu.make_async_copy(lower_half, lower_half, recv_sem.at[0])
+        pl.when(level == jnp.where(z < half, 0, half - 1))(together.wait)
         for group in range(0, line, RASTER):
             lefts, rights = [], []
             for source in range(group, min(group + RASTER, line)):
@@ -217,12 +237,12 @@
     tile = lax.fori_loop(0, depth, raster, jnp.zeros((TR, TC), F32))
     part[...] = tile.reshape(reps, quarter, TC)
 
-    for k in range(1, reps):
+    for k in sorted(range(1, reps), key=lambda k: -min(k, reps - k)):
         peer = lax.rem(r + k, reps)
         pltpu.make_async_remote_copy(
             src_ref=part.at[peer],
             dst_ref=gathered.at[k - 1],
-            send_sem=part_send_sem,
+            send_sem=in_sem,
             recv_sem=part_recv_sem,
             device_id={"files": f, "rep": peer},
             device_id_type=MESH,
@@ -235,7 +255,7 @@
 
     sent = send.at[pl.ds(0, 2 * (files - 1))]
     pltpu.make_async_copy(sent, sent, send_sem).wait()
-    pltpu.make_async_copy(gathered, gathered, part_send_sem).wait()
+    pltpu.make_async_copy(gathered, gathered, in_sem).wait()
 
 
 def solution(mesh):
@@ -255,15 +275,14 @@
                 pltpu.VMEM((3, blocks, LANES), jnp.int32),
                 pltpu.VMEM((blocks, LANES), BF),
                 pltpu.VMEM((3, blocks, LANES), F32),
-                pltpu.VMEM((2 * files, CAP), F32),
+                pltpu.VMEM((2 * files + SUB, CAP), F32),
                 pltpu.VMEM((depth, files // depth, 2, CAP), F32),
                 pltpu.VMEM((reps, TR // reps, TC), F32),
                 pltpu.VMEM((reps - 1, TR // reps, TC), F32),
-                pltpu.SemaphoreType.DMA((2,)),
                 pltpu.SemaphoreType.DMA,
-                pltpu.SemaphoreType.DMA((depth,)),
-                pltpu.SemaphoreType.REGULAR((depth,)),
                 pltpu.SemaphoreType.DMA,
+                pltpu.SemaphoreType.DMA((depth - depth // 2 + 1,)),
+                pltpu.SemaphoreType.REGULAR((2 + (depth - depth // 2 - 1) // 2,)),
                 pltpu.SemaphoreType.DMA,
             ],
             compiler_params=pltpu.CompilerParams(

time: 26 us -> 25.8 us (level)
  no operation moved by 1% of the time
where the time goes in v5:
time: 25.8 us; the launch traced here: 25.7 us
  Pallas kernels  25.1 us (97%)
  local copies, waits for them, and re-layouts  0.6 us (2%)
    pallas_call x1, Pallas kernels, per_device(): pl.pallas_call(functools.partial(kernel, files, reps), out_shape=jax.Shap...  25.1 us
    unnamed x1, local copies, waits for them, and re-layouts  0.6 us

profile of v5, /device:TPU:1, one launch (start us, length us, event | category | flops | bytes accessed | tf_op | source)
XLA Modules:
  0.0 25.7 jit_solution(14766732229668976611)
XLA Ops:
  0.0 25.1 %shard_map.46 = f32[8,128]{1,0:T(8,128)S(1)} custom-call(s32[32,128]{1,0:T(8,128)} %bitcast.6, s32[32,128]{1,0:T(8,128)} %bitcast.7, s32[32,128]{1,0:T(8,128)} %bitcast.8, bf16[32,128]{1,0:T(8,128)(2,1)} %bitcast.9), custom_call_target="tpu_custom_call" | custom-call | tf_op jit(solution)/shard_map/pallas_call | solution.py:269
  25.1 0.6 %copy.6 = f32[1,8,128]{2,1,0:T(8,128)} copy(f32[1,8,128]{2,1,0:T(8,128)S(1)} %bitcast.5) | data formatting | bytes 8192
